TPU v7x, 32 devices: a whole 2x2x4 slice. The times are simulated.
32 devices in a mesh: expert: 4 (over x, core), shard: 8 (over z, y).
Axes of the slice: x: 2, y: 2, z: 4, core: 2. Of those that a mesh axis runs over, the one named last changes fastest.
Arguments:
- w_gate: float32 [64, 2048, 1408], P('expert', 'shard'), may hold values from -0.1875 to 0.1875
- w_up: float32 [64, 2048, 1408], P('expert', 'shard'), may hold values from -0.1875 to 0.1875
- router_weight: float32 [2048, 64], P('shard', 'expert'), may hold values from -0.125 to 0.125
- router_gain: float32 [2048], P('shard'), may hold values from 0.25 to 1.75
Outputs:
- serve_gate: bfloat16 [64, 2048, 1408], P('expert', None, 'shard')
- serve_up: bfloat16 [64, 2048, 1408], P('expert', None, 'shard')
- scale_gate: float32 [64, 1408], P('expert', 'shard')
- scale_up: float32 [64, 1408], P('expert', 'shard')
- serve_router: bfloat16 [2048, 64], replicated
All inputs are finite; a program needn't handle non-finite values. Where the computation divides by a largest or mean magnitude, that divisor is 1e-20 or more.
Results may differ from a plain program's by a relative error of at most 0.001.
Values may be sent and summed in bfloat16 or wider, within the bound.
A program may use at most 192 MiB of HBM per device.

v0:
```python
import jax
import jax.numpy as jnp
from jax import lax
from jax.sharding import PartitionSpec as P

D_MODEL = 2048


def on_device(w_gate, w_up, router_weight, router_gain):
    total_gate, total_up = lax.psum(
        (jnp.sum(jnp.abs(w_gate), axis=1), jnp.sum(jnp.abs(w_up), axis=1)), "shard"
    )
    scale_gate = total_gate / D_MODEL
    scale_up = total_up / D_MODEL
    narrow_gate, narrow_up = (
        (w_gate / jnp.expand_dims(scale_gate, 1)).astype(jnp.bfloat16),
        (w_up / jnp.expand_dims(scale_up, 1)).astype(jnp.bfloat16),
    )
    serve_gate, serve_up = (
        lax.all_to_all(narrow_gate, "shard", split_axis=2, concat_axis=1, tiled=True),
        lax.all_to_all(narrow_up, "shard", split_axis=2, concat_axis=1, tiled=True),
    )
    scale_gate = lax.dynamic_slice_in_dim(
        scale_gate, lax.axis_index("shard") * serve_gate.shape[2], serve_gate.shape[2], axis=1
    )
    scale_up = lax.dynamic_slice_in_dim(
        scale_up, lax.axis_index("shard") * serve_up.shape[2], serve_up.shape[2], axis=1
    )
    part_router = (router_weight * router_gain[:, None]).astype(jnp.bfloat16)
    row_router = lax.all_gather(part_router, "shard", axis=0, tiled=True)
    serve_router = lax.all_gather(row_router, "expert", axis=1, tiled=True)
    return (serve_gate, serve_up, scale_gate, scale_up, serve_router)


def solution(mesh):
    placed = (
        P("expert", "shard", None),
        P("expert", "shard", None),
        P("shard", "expert"),
        P("shard"),
    )
    return jax.shard_map(
        on_device,
        mesh=mesh,
        in_specs=placed,
        out_specs=(
            P("expert", None, "shard"),
            P("expert", None, "shard"),
            P("expert", "shard"),
            P("expert", "shard"),
            P(),
        ),
        check_vma=False,
    )
```

profile of v0, /device:TPU:0, one launch (start us, length us, event | category | flops | bytes accessed | tf_op | source)
XLA Modules:
  0.0 714.1 jit_solution(9484981068573006527)
XLA Ops:
  7.2 0.0 all-reduce.3.cloned.1.call-start
  7.2 16.0 %abs_reduce_fusion = (f32[16,1408]{1,0:T(8,128)}, f32[16,1408]{1,0:T(8,128)}) fusion(f32[16,256,1408]{2,1,0:T(8,128)} %param.5, f32[16,256,1408]{2,1,0:T(8,128)} %param.4), kind=kLoop, calls=%fused_computation.1 | loop fusion | flops 23023616 | bytes 46317568 | tf_op jit(solution)/shard_map/reduce_sum | solution.py:11
  23.3 0.0 all-reduce.3.cloned.1.call-update
  23.3 23.7 %copy.22 = f32[16,256,1408]{1,0,2:T(8,128)} copy(f32[16,256,1408]{2,1,0:T(8,128)} %param.5) | data formatting | bytes 46137344 | tf_op args[1]
  47.0 50.0 %all-reduce.3.cloned.1.call-done = (f32[16,1408]{1,0:T(8,128)}, f32[16,1408]{1,0:T(8,128)}) async-done(((f32[16,1408]{1,0:T(8,128)}, f32[16,1408]{1,0:T(8,128)}), (f32[16,1408]{1,0:T(8,128)}, f32[16,1408]{1,0:T(8,128)})) %all-reduce.3.cloned.1.call-update) | async-done | bytes 180240 | tf_op jit(solution)/shard_map/psum | solution.py:10
  97.0 0.9 broadcast_multiply_fusion
  97.9 0.3 copy.21
  98.1 14.2 %divide_convert_fusion = bf16[16,256,1408]{1,0,2:T(8,128)(2,1)} fusion(f32[16,256,1408]{1,0,2:T(8,128)} %copy.22, f32[16,1408]{0,1:T(8,128)S(1)} %copy.21), kind=kLoop, calls=%fused_computation | loop fusion | flops 11534336 | bytes 34693120 | tf_op jit(solution)/shard_map/convert_element_type | solution.py:17
  112.4 5.2 all-to-all-start.1
  117.6 0.0 copy-start
  117.6 23.7 %copy.18 = f32[16,256,1408]{1,0,2:T(8,128)} copy(f32[16,256,1408]{2,1,0:T(8,128)} %param.4) | data formatting | bytes 46137344 | tf_op args[0]
  141.3 0.0 copy-done
  141.3 0.3 copy.17
  141.6 0.0 copy-start.1
  141.6 0.0 copy-start.2
  141.6 14.2 %divide_convert_fusion.1 = bf16[16,256,1408]{1,0,2:T(8,128)(2,1)} fusion(f32[16,256,1408]{1,0,2:T(8,128)} %copy.18, f32[16,1408]{0,1:T(8,128)S(1)} %copy.17), kind=kLoop, calls=%fused_computation.2 | loop fusion | flops 11534336 | bytes 34693120 | tf_op jit(solution)/shard_map/convert_element_type | solution.py:16
  155.8 210.5 %all-to-all-done.1 = bf16[16,256,1408]{1,0,2:T(8,128)(2,1)} async-done(((bf16[16,256,1408]{1,0,2:T(8,128)(2,1)}), bf16[16,256,1408]{1,0,2:T(8,128)(2,1)}, u32[]{:S(2)}, u32[]{:S(2)}) %all-to-all-start.1) | async-done | bytes 11534368 | tf_op jit(solution)/shard_map/all_to_all | solution.py:21
  366.4 5.3 all-to-all-start
  371.7 0.0 copy-done.1
  371.7 0.0 copy-done.2
  371.7 269.1 %all_gather.6 = bf16[2048,16]{0,1:T(8,128)(2,1)S(1)} all-gather(bf16[256,16]{0,1:T(8,128)(2,1)S(1)} %multiply_convert_fusion), channel_id=1, replica_groups=mesh['expert'=4,'shard'=8] {'shard'}, dimensions={0}, use_global_device_ids=true | all-gather | bytes 73728 | tf_op jit(solution)/shard_map/all_gather | solution.py:30
  640.8 5.8 all_gather.7
  646.6 0.7 constant_dynamic-slice_fusion
  647.3 0.7 constant_dynamic-slice_fusion.1
  647.9 11.4 %copy.24 = bf16[16,8,256,176]{2,1,3,0:T(8,128)(2,1)} copy(bf16[16,8,256,176]{2,0,3,1:T(8,128)(2,1)} %bitcast.5) | data formatting | bytes 23068672 | tf_op jit(solution)/shard_map/all_to_all | solution.py:21
  659.3 18.0 %all_to_all.33 = bf16[16,2048,176]{1,2,0:T(8,128)(2,1)} reshape(bf16[16,8,256,176]{2,1,3,0:T(8,128)(2,1)} %copy.24) | data formatting | bytes 23068672 | tf_op jit(solution)/shard_map/all_to_all | solution.py:21
  677.3 0.0 all-to-all-done
  677.3 11.4 %copy.20 = bf16[16,8,256,176]{2,1,3,0:T(8,128)(2,1)} copy(bf16[16,8,256,176]{2,0,3,1:T(8,128)(2,1)} %bitcast.2) | data formatting | bytes 23068672 | tf_op jit(solution)/shard_map/all_to_all | solution.py:20
  688.6 18.0 %all_to_all.29 = bf16[16,2048,176]{1,2,0:T(8,128)(2,1)} reshape(bf16[16,8,256,176]{2,1,3,0:T(8,128)(2,1)} %copy.20) | data formatting | bytes 23068672 | tf_op jit(solution)/shard_map/all_to_all | solution.py:20
  706.6 0.7 copy.30
  (2 shorter events, 0.0 us)
Async XLA Ops:
  7.2 89.8 %all-reduce.3.cloned.1.call-start = ((), (), s32[]{:S(2)}) async-start(), calls=%async_computation.2 | async-start | bytes 360448 | tf_op jit(solution)/shard_map/psum | solution.py:10
  112.4 254.0 %all-to-all-start.1 = ((bf16[16,256,1408]{1,0,2:T(8,128)(2,1)}), bf16[16,256,1408]{1,0,2:T(8,128)(2,1)}, u32[]{:S(2)}, u32[]{:S(2)}) async-start(bf16[16,256,1408]{1,0,2:T(8,128)(2,1)} %divide_convert_fusion), calls=%async_computation.1 | async-start | bytes 23068672 | tf_op jit(solution)/shard_map/all_to_all | solution.py:21
  117.6 23.7 %copy-start = (f32[16,1408]{1,0:T(8,128)S(1)}, f32[16,1408]{1,0:T(8,128)}, u32[]{:S(2)}) copy-start(f32[16,1408]{1,0:T(8,128)} %get-tuple-element.5) | copy-start | bytes 270340
  141.6 230.1 %copy-start.1 = (f32[256,16]{0,1:T(8,128)S(1)}, f32[256,16]{0,1:T(8,128)}, u32[]{:S(2)}) copy-start(f32[256,16]{0,1:T(8,128)} %param.6) | copy-start | bytes 49156
  141.6 230.1 %copy-start.2 = (f32[256]{0:T(256)S(1)}, f32[256]{0:T(256)}, u32[]{:S(2)}) copy-start(f32[256]{0:T(256)} %param.7) | copy-start | bytes 3076
  366.4 310.9 %all-to-all-start = ((bf16[16,256,1408]{1,0,2:T(8,128)(2,1)}), bf16[16,256,1408]{1,0,2:T(8,128)(2,1)}, u32[]{:S(2)}, u32[]{:S(2)}) async-start(bf16[16,256,1408]{1,0,2:T(8,128)(2,1)} %divide_convert_fusion.1), calls=%async_computation | async-start | bytes 23068672 | tf_op jit(solution)/shard_map/all_to_all | solution.py:20
Sparse Core Ops, SparseCore 0:
  23.4 73.5 all-reduce.2
where the time goes:
time: 716 us; the launch traced here: 714 us
  blocking collectives  275 us (38%)
  waiting for transfers between devices  261 us (36%)
  local copies, waits for them, and re-layouts  109 us (15%)
  other arithmetic  45.4 us (6%)
  between operations  14.1 us (2%)
  starting transfers between devices  10.5 us (1%)
    all_gather x1, blocking collectives, on_device(): row_router = lax.all_gather(part_router, 'shard', axis=0, tiled=True)  269 us
    all_to_all x1, waiting for transfers between devices, on_device(): lax.all_to_all(narrow_up, 'shard', split_axis=2, concat_axis=1, tiled=True)  211 us
    psum x1, waiting for transfers between devices, on_device(): lax.psum((jnp.sum(jnp.abs(w_gate), axis=1), jnp.sum(jnp.abs(w_up), axis=1...  50 us
    unnamed x9, local copies, waits for them, and re-layouts  48.1 us
    all_to_all x2, local copies, waits for them, and re-layouts, on_device(): lax.all_to_all(narrow_gate, 'shard', split_axis=2, concat_axis=1, tiled=T...  29.3 us
    all_to_all x2, local copies, waits for them, and re-layouts, on_device(): lax.all_to_all(narrow_up, 'shard', split_axis=2, concat_axis=1, tiled=True)  29.3 us
    reduce_sum x1, other arithmetic, on_device(): jnp.sum(jnp.abs(w_up), axis=1)  16 us
  transfers between devices with their start and end apart: 3, of which 2 were waited for; matrix products, arithmetic and copies ran while one was open for 10% of the time, Pallas kernels for 0%

commit v1 on v0

--- a/solution.py
+++ b/solution.py
@@ -4,6 +4,12 @@
 from jax.sharding import PartitionSpec as P
 
 D_MODEL = 2048
+cards_view = lambda content: jnp.concatenate(
+    lax.all_to_all(
+        jnp.stack(jnp.split(content, lax.axis_size("shard"), axis=2), axis=0), "shard", 0, 0
+    ),
+    axis=1,
+)
 
 
 def on_device(w_gate, w_up, router_weight, router_gain):
@@ -18,7 +24,7 @@
     )
     serve_gate, serve_up = (
         lax.all_to_all(narrow_gate, "shard", split_axis=2, concat_axis=1, tiled=True),
-        lax.all_to_all(narrow_up, "shard", split_axis=2, concat_axis=1, tiled=True),
+        cards_view(narrow_up),
     )
     scale_gate = lax.dynamic_slice_in_dim(
         scale_gate, lax.axis_index("shard") * serve_gate.shape[2], serve_gate.shape[2], axis=1

time: 716 us -> 697 us (0.973)
  local copies, waits for them, and re-layouts: 109 us -> 98.4 us
    all_to_all x1, waiting for transfers between devices: 211 us -> 0.01 us  [lax.all_to_all(jnp.stack(jnp.split(content, lax.axis_size('shard'), axis=...]
    all_to_all x1, waiting for transfers between devices: 0.01 us -> 206 us  [on_device(): lax.all_to_all(narrow_gate, 'shard', split_axis=2, concat_axis=1, tiled=T...]
    all_to_all x2 -> x0, local copies, waits for them, and re-layouts: 29.3 us -> none  [on_device(): lax.all_to_all(narrow_up, 'shard', split_axis=2, concat_axis=1, tiled=True)]
    reshape x0 -> x1, local copies, waits for them, and re-layouts: none -> 10 us  [jnp.concatenate(lax.all_to_all(jnp.stack(jnp.split(content, lax.axis_size...]
    unnamed x9 -> x16, local copies, waits for them, and re-layouts: 48.1 us -> 56.2 us
  transfers between devices with their start and end apart: 3 -> 3, of which waited for: 2 -> 2; matrix products, arithmetic and copies ran while one was open for 10% -> 11% of each run, Pallas kernels for 0% -> 0%
where the time goes in v1:
time: 697 us; the launch traced here: 695 us
  blocking collectives  275 us (39%)
  waiting for transfers between devices  256 us (37%)
  local copies, waits for them, and re-layouts  98.4 us (14%)
  other arithmetic  41 us (6%)
  between operations  14.1 us (2%)
  starting transfers between devices  10.5 us (2%)
    all_gather x1, blocking collectives, on_device(): row_router = lax.all_gather(part_router, 'shard', axis=0, tiled=True)  269 us
    all_to_all x1, waiting for transfers between devices, on_device(): lax.all_to_all(narrow_gate, 'shard', split_axis=2, concat_axis=1, tiled=T...  206 us
    unnamed x16, local copies, waits for them, and re-layouts  56.2 us
    psum x1, waiting for transfers between devices, on_device(): lax.psum((jnp.sum(jnp.abs(w_gate), axis=1), jnp.sum(jnp.abs(w_up), axis=1...  50 us
    all_to_all x2, local copies, waits for them, and re-layouts, on_device(): lax.all_to_all(narrow_gate, 'shard', split_axis=2, concat_axis=1, tiled=T...  29.3 us
    reduce_sum x1, other arithmetic, on_device(): jnp.sum(jnp.abs(w_up), axis=1)  16 us
    convert_element_type x1, other arithmetic, on_device(): (w_gate / jnp.expand_dims(scale_gate, 1)).astype(jnp.bfloat16)  14.2 us
  transfers between devices with their start and end apart: 3, of which 2 were waited for; matrix products, arithmetic and copies ran while one was open for 11% of the time, Pallas kernels for 0%

profile of v1, /device:TPU:0, one launch (start us, length us, event | category | flops | bytes accessed | tf_op | source)
XLA Modules:
  0.0 694.8 jit_solution(5658346022208422891)
XLA Ops:
  7.2 0.0 all-reduce.3.cloned.1.call-start
  7.2 16.0 %abs_reduce_fusion = (f32[16,1408]{1,0:T(8,128)}, f32[16,1408]{1,0:T(8,128)}) fusion(f32[16,256,1408]{2,1,0:T(8,128)} %param.5, f32[16,256,1408]{2,1,0:T(8,128)} %param.4), kind=kLoop, calls=%fused_computation.1 | loop fusion | flops 23023616 | bytes 46317568 | tf_op jit(solution)/shard_map/reduce_sum | solution.py:17
  23.3 0.0 all-reduce.3.cloned.1.call-update
  23.3 23.7 %copy.22 = f32[16,256,1408]{1,0,2:T(8,128)} copy(f32[16,256,1408]{2,1,0:T(8,128)} %param.4) | data formatting | bytes 46137344 | tf_op args[0]
  47.0 50.0 %all-reduce.3.cloned.1.call-done = (f32[16,1408]{1,0:T(8,128)}, f32[16,1408]{1,0:T(8,128)}) async-done(((f32[16,1408]{1,0:T(8,128)}, f32[16,1408]{1,0:T(8,128)}), (f32[16,1408]{1,0:T(8,128)}, f32[16,1408]{1,0:T(8,128)})) %all-reduce.3.cloned.1.call-update) | async-done | bytes 180240 | tf_op jit(solution)/shard_map/psum | solution.py:16
  97.0 0.9 broadcast_multiply_fusion.1
  97.9 0.3 copy.21
  98.1 14.2 %divide_convert_fusion.1 = bf16[16,256,1408]{1,0,2:T(8,128)(2,1)} fusion(f32[16,256,1408]{1,0,2:T(8,128)} %copy.22, f32[16,1408]{0,1:T(8,128)S(1)} %copy.21), kind=kLoop, calls=%fused_computation.2 | loop fusion | flops 11534336 | bytes 34693120 | tf_op jit(solution)/shard_map/convert_element_type | solution.py:22
  112.4 5.2 all-to-all-start
  117.6 0.0 copy-start
  117.6 23.4 %copy.25 = f32[16,256,1408]{1,2,0:T(8,128)} copy(f32[16,256,1408]{2,1,0:T(8,128)} %param.5) | data formatting | bytes 46137344 | tf_op args[1]
  141.0 0.0 copy-done
  141.0 9.8 %divide_convert_fusion = bf16[16,256,1408]{1,2,0:T(8,128)(2,1)S(1)} fusion(f32[16,256,1408]{1,2,0:T(8,128)} %copy.25, f32[16,1408]{1,0:T(8,128)S(1)} %broadcast_multiply_fusion), kind=kLoop, calls=%fused_computation | loop fusion | flops 11534336 | bytes 34693120 | tf_op jit(solution)/shard_map/convert_element_type | solution.py:23
  150.8 1.2 fusion.7
  152.0 1.2 fusion.6
  153.3 1.2 fusion.5
  154.5 1.2 fusion.4
  155.7 1.2 fusion.3
  156.9 1.2 fusion.2
  158.1 1.2 fusion.1
  159.3 1.2 fusion
  160.5 0.0 copy-start.1
  160.5 0.0 copy-start.2
  160.5 205.9 %all-to-all-done = bf16[16,256,1408]{1,0,2:T(8,128)(2,1)} async-done(((bf16[16,256,1408]{1,0,2:T(8,128)(2,1)}), bf16[16,256,1408]{1,0,2:T(8,128)(2,1)}, u32[]{:S(2)}, u32[]{:S(2)}) %all-to-all-start) | async-done | bytes 11534368 | tf_op jit(solution)/shard_map/all_to_all | solution.py:26
  366.4 5.3 all-to-all-start.1
  371.7 0.0 copy-done.1
  371.7 0.0 copy-done.2
  371.7 269.1 %all_gather.6 = bf16[2048,16]{0,1:T(8,128)(2,1)S(1)} all-gather(bf16[256,16]{0,1:T(8,128)(2,1)S(1)} %multiply_convert_fusion), channel_id=1, replica_groups=mesh['expert'=4,'shard'=8] {'shard'}, dimensions={0}, use_global_device_ids=true | all-gather | bytes 73728 | tf_op jit(solution)/shard_map/all_gather | solution.py:36
  640.8 5.8 all_gather.7
  646.6 0.7 constant_dynamic-slice_fusion.1
  647.3 0.7 constant_dynamic-slice_fusion
  647.9 11.3 %copy.24 = bf16[16,8,256,176]{2,1,3,0:T(8,128)(2,1)} copy(bf16[16,8,256,176]{2,0,3,1:T(8,128)(2,1)} %bitcast.2) | data formatting | bytes 23068672 | tf_op jit(solution)/shard_map/all_to_all | solution.py:26
  659.3 18.0 %all_to_all.19 = bf16[16,2048,176]{1,2,0:T(8,128)(2,1)} reshape(bf16[16,8,256,176]{2,1,3,0:T(8,128)(2,1)} %copy.24) | data formatting | bytes 23068672 | tf_op jit(solution)/shard_map/all_to_all | solution.py:26
  677.2 0.0 all-to-all-done.1
  677.2 10.0 %copy.28 = bf16[8,16,22,8,256]{4,3,0,2,1:T(8,128)(2,1)} copy(bf16[8,16,22,8,256]{4,3,2,1,0:T(8,128)(2,1)} %bitcast.12) | data formatting | bytes 23068672 | tf_op jit(solution)/shard_map/reshape | solution.py:7
  687.2 0.7 copy.39
  (2 shorter events, 0.0 us)
Async XLA Ops:
  7.2 89.8 %all-reduce.3.cloned.1.call-start = ((), (), s32[]{:S(2)}) async-start(), calls=%async_computation.2 | async-start | bytes 360448 | tf_op jit(solution)/shard_map/psum | solution.py:16
  112.4 254.0 %all-to-all-start = ((bf16[16,256,1408]{1,0,2:T(8,128)(2,1)}), bf16[16,256,1408]{1,0,2:T(8,128)(2,1)}, u32[]{:S(2)}, u32[]{:S(2)}) async-start(bf16[16,256,1408]{1,0,2:T(8,128)(2,1)} %divide_convert_fusion.1), calls=%async_computation | async-start | bytes 23068672 | tf_op jit(solution)/shard_map/all_to_all | solution.py:26
  117.6 23.4 %copy-start = (f32[16,1408]{1,0:T(8,128)S(1)}, f32[16,1408]{1,0:T(8,128)}, u32[]{:S(2)}) copy-start(f32[16,1408]{1,0:T(8,128)} %get-tuple-element.6) | copy-start | bytes 270340
  160.5 211.2 %copy-start.1 = (f32[256,16]{0,1:T(8,128)S(1)}, f32[256,16]{0,1:T(8,128)}, u32[]{:S(2)}) copy-start(f32[256,16]{0,1:T(8,128)} %param.6) | copy-start | bytes 49156
  160.5 211.2 %copy-start.2 = (f32[256]{0:T(256)S(1)}, f32[256]{0:T(256)}, u32[]{:S(2)}) copy-start(f32[256]{0:T(256)} %param.7) | copy-start | bytes 3076
  366.4 310.9 %all-to-all-start.1 = ((bf16[8,16,256,176]{2,3,1,0:T(8,128)(2,1)}), bf16[8,16,256,176]{2,3,1,0:T(8,128)(2,1)}, u32[]{:S(2)}, u32[]{:S(2)}) async-start(bf16[8,16,256,176]{2,3,1,0:T(8,128)(2,1)} %fusion), calls=%async_computation.1 | async-start | bytes 23068672 | tf_op jit(solution)/shard_map/all_to_all | solution.py:8
Sparse Core Ops, SparseCore 0:
  23.4 73.5 all-reduce.2
